TPU v7x, 32 devices: a whole 2x2x4 slice. The times are simulated.
32 devices in a mesh: front: 8 (over y, x, core), sub: 4 (over z).
Axes of the slice: x: 2, y: 2, z: 4, core: 2. Of those that a mesh axis runs over, the one named last changes fastest.
Arguments:
- row_values: float32 [4096, 1024], P(('front', 'sub')), may hold values from -0.12 to 0.12
- front_of_row: int32 [4096, 1], P(('front', 'sub')), may hold values from 0 to 7; in each aligned block of 128 rows (0 to 127, 128 to 255, ...) at most 32 rows name the same one
- child_factors: float32 [16, 512, 512], P('front', 'sub'), as said below
- child_columns: int32 [16, 512], P('front'), may hold values from 0 to 1023, as said below
- damping: float32 [8, 1024], P('front'), may hold values from 0.5 to 2
Outputs:
- front_factor: float32 [8, 1024, 1024], P('front', 'sub')
Inputs may be any that keep to these rules, and one draw needn't show every extreme that they name: `front_of_row`: among the 128 rows of one device, at most 32 name the same front, and some device's block reaches this bound. `child_factors`: each block is upper triangular with a positive diagonal. `child_columns`: each row names 512 distinct columns.
All inputs are finite; a program needn't handle non-finite values.
Results may differ from a plain program's by a relative error of at most 0.0003.
Values sent between devices are 32-bit elements; how exact they have to be, the bound alone decides.
A program may use at most 64 MiB of HBM per device.

v0:
```python
import jax
import jax.numpy as jnp
from jax import lax
from jax.sharding import PartitionSpec as P

HIGHEST = lax.Precision.HIGHEST


def cross_product(left_cols, right_cols):
    return lax.dot_general(
        left_cols,
        right_cols,
        (((0,), (0,)), ((), ())),
        precision=HIGHEST,
        preferred_element_type=jnp.float32,
    )


def local(row_values, front_of_row, child_factors, child_columns, damping):
    fronts = lax.axis_size("front")
    rows_held, front_width = row_values.shape
    capacity = 2 * rows_held // fronts
    destination = front_of_row[:, 0]
    onehot = (destination[:, None] == jnp.arange(fronts, dtype=jnp.int32)[None, :]).astype(
        jnp.int32
    )
    position = jnp.sum((jnp.cumsum(onehot, axis=0) - onehot) * onehot, axis=1)
    slot_of = destination * capacity + position
    source = (
        jnp.full((fronts * capacity,), rows_held, jnp.int32)
        .at[slot_of]
        .set(jnp.arange(rows_held, dtype=jnp.int32))
    )
    padded = jnp.concatenate([row_values, jnp.zeros((1, front_width), row_values.dtype)], axis=0)
    outgoing = padded[source]
    received = lax.all_to_all(outgoing, "front", split_axis=0, concat_axis=0, tiled=True)
    columns = jnp.arange(front_width, dtype=jnp.int32)
    spread = (child_columns[:, :, None] == columns[None, None, :]).astype(jnp.float32)
    placed = jnp.einsum(
        "jrc,jcf->jrf", child_factors, spread, precision=HIGHEST, preferred_element_type=jnp.float32
    )
    stacked = jnp.concatenate([placed.reshape(-1, front_width), received], axis=0)
    sub_count = lax.axis_size("sub")
    block_rows = front_width // sub_count
    own_index = lax.axis_index("sub")
    weight = damping[0]
    summed_gram = lax.psum(cross_product(stacked, stacked), "sub")
    summed_gram = summed_gram + jnp.diag(weight * weight)
    full_factor = jnp.linalg.cholesky(summed_gram).T
    own_rows = lax.dynamic_slice_in_dim(full_factor, own_index * block_rows, block_rows, 0)
    return own_rows[None]


def solution(mesh):
    in_specs = (
        P(("front", "sub"), None),
        P(("front", "sub"), None),
        P("front", "sub", None),
        P("front", None),
        P("front", None),
    )
    out_specs = P("front", "sub", None)
    return jax.shard_map(local, mesh=mesh, in_specs=in_specs, out_specs=out_specs, check_vma=False)
```

profile of v0, /device:TPU:0, one launch (start us, length us, event | category | flops | bytes accessed | tf_op | source)
XLA Modules:
  0.0 432.0 jit_solution(13834568773688344293)
XLA Ops:
  6.5 0.8 fusion.36
  7.3 0.2 reduce_window_sum.11
  7.5 0.8 select_reduce_fusion.8
  8.3 0.7 fusion.37
  9.0 1.0 scatter_custom_fusion
  10.0 1.1 concatenate.6
  11.1 2.0 gather_fusion
  13.1 5.2 %all-to-all-start = ((f32[8,32,1024]{2,1,0:T(8,128)}), f32[8,32,1024]{2,1,0:T(8,128)S(1)}, u32[]{:S(2)}, u32[]{:S(2)}) async-start(f32[8,32,1024]{2,1,0:T(8,128)} %bitcast.5), calls=%async_computation | async-start | bytes 2097152 | tf_op jit(solution)/shard_map/all_to_all | solution.py:36
  18.4 1.6 fusion.1
  20.0 13.7 %all-to-all-done = f32[8,32,1024]{2,1,0:T(8,128)S(1)} async-done(((f32[8,32,1024]{2,1,0:T(8,128)}), f32[8,32,1024]{2,1,0:T(8,128)S(1)}, u32[]{:S(2)}, u32[]{:S(2)}) %all-to-all-start) | async-done | bytes 1048608 | tf_op jit(solution)/shard_map/all_to_all | solution.py:36
  33.7 8.4 %fusion.2 = f32[1024,1024]{0,1:T(8,128)} fusion(f32[256,1024]{1,0:T(8,128)S(1)} %bitcast.58, f32[256,1024]{1,0:T(8,128)S(1)} %bitcast.63), kind=kOutput, calls=%fused_computation.8 | convolution fusion | flops 6442975232 | bytes 6291456 | tf_op jit(solution)/shard_map/dot_general | solution.py:10
  42.2 0.7 copy-done.2
  42.9 153.9 %all-reduce.4.cloned.1.call-done = f32[1024,1024]{0,1:T(8,128)} async-done(((f32[1024,1024]{0,1:T(8,128)}), f32[1024,1024]{0,1:T(8,128)}) %all-reduce.4.cloned.1.call-update) | async-done | bytes 4194320 | tf_op jit(solution)/shard_map/psum | solution.py:47
  196.7 4.8 %select_add_fusion = f32[1024,1024]{0,1:T(8,128)} fusion(f32[1024,1024]{0,1:T(8,128)} %all-reduce.4.cloned.1.call-done, f32[1024]{0:T(1024)S(1)} %bitcast.59), kind=kLoop, calls=%fused_computation.4 | loop fusion | flops 3145728 | bytes 8392704 | tf_op jit(solution)/shard_map/add | solution.py:48
  201.6 5.5 %copy.7 = f32[1024,1024]{1,0:T(8,128)} copy(f32[1024,1024]{0,1:T(8,128)} %select_add_fusion) | data formatting | bytes 8388608 | tf_op jit(solution)/shard_map/add | solution.py:48
  207.1 4.4 %fusion = f32[1024,1024]{1,0:T(8,128)S(1)} fusion(f32[1024,1024]{1,0:T(8,128)} %copy.7, f32[1024,1024]{0,1:T(8,128)} %all-reduce.4.cloned.1.call-done, f32[1024]{0:T(1024)S(1)} %bitcast.60), kind=kLoop, calls=%fused_computation.3 | loop fusion | flops 5242880 | bytes 12587008 | tf_op jit(solution)/shard_map/jit(cholesky)/div | solution.py:49
  211.6 1.9 copy-done.1
  213.5 11.7 %cholesky.224 = f32[128,128]{1,0:T(8,128)S(1)} custom-call(f32[128,128]{1,0:T(8,128)S(1)} %cholesky.580), custom_call_target="Cholesky" | custom-call | tf_op jit(solution)/shard_map/jit(cholesky)/cholesky | solution.py:49
  225.4 9.8 %custom-call.59 = f32[1,128,128]{1,2,0:T(8,128)S(1)} custom-call(f32[1,128,128]{2,1,0:T(8,128)S(1)} %get-tuple-element.18), custom_call_target="InvertDiagBlocksLowerTriangular" | custom-call | tf_op jit(solution)/shard_map/jit(cholesky)/cholesky | solution.py:49
  235.2 1.5 fusion.15
  236.7 0.2 copy.9
  236.9 1.6 convolution_subtract_fusion
  238.5 11.7 %cholesky.245 = f32[128,128]{1,0:T(8,128)S(1)} custom-call(f32[128,128]{1,0:T(8,128)S(1)} %cholesky.584), custom_call_target="Cholesky" | custom-call | tf_op jit(solution)/shard_map/jit(cholesky)/cholesky | solution.py:49
  250.7 2.5 cholesky.256
  253.2 9.8 %custom-call.60 = f32[1,128,128]{1,2,0:T(8,128)S(1)} custom-call(f32[1,128,128]{2,1,0:T(8,128)S(1)} %get-tuple-element.16), custom_call_target="InvertDiagBlocksLowerTriangular" | custom-call | tf_op jit(solution)/shard_map/jit(cholesky)/cholesky | solution.py:49
  263.0 0.8 constant_dynamic-update-slice_fusion.7
  263.9 0.6 constant_dynamic-update-slice_fusion.6
  264.5 1.3 convolution_dynamic-update-slice_fusion
  265.8 2.7 convolution_subtract_fusion.1
  268.5 11.7 %cholesky.469 = f32[128,128]{1,0:T(8,128)S(1)} custom-call(f32[128,128]{1,0:T(8,128)S(1)} %cholesky.589), custom_call_target="Cholesky" | custom-call | tf_op jit(solution)/shard_map/jit(cholesky)/cholesky | solution.py:49
  280.4 0.6 constant_dynamic-update-slice_fusion.5
  281.0 9.8 %custom-call.61 = f32[1,128,128]{1,2,0:T(8,128)S(1)} custom-call(f32[1,128,128]{2,1,0:T(8,128)S(1)} %get-tuple-element.14), custom_call_target="InvertDiagBlocksLowerTriangular" | custom-call | tf_op jit(solution)/shard_map/jit(cholesky)/cholesky | solution.py:49
  290.8 1.3 convolution_dynamic-update-slice_fusion.1
  292.1 3.3 convolution_subtract_fusion.2
  295.4 11.7 %cholesky.488 = f32[128,128]{1,0:T(8,128)S(1)} custom-call(f32[128,128]{1,0:T(8,128)S(1)} %cholesky.594), custom_call_target="Cholesky" | custom-call | tf_op jit(solution)/shard_map/jit(cholesky)/cholesky | solution.py:49
  307.3 0.6 constant_dynamic-update-slice_fusion.3
  307.9 9.8 %custom-call.62 = f32[1,128,128]{1,2,0:T(8,128)S(1)} custom-call(f32[1,128,128]{2,1,0:T(8,128)S(1)} %get-tuple-element.12), custom_call_target="InvertDiagBlocksLowerTriangular" | custom-call | tf_op jit(solution)/shard_map/jit(cholesky)/cholesky | solution.py:49
  317.7 1.1 convolution_dynamic-update-slice_fusion.2
  318.8 3.1 convolution_subtract_fusion.3
  322.0 11.9 %cholesky.507 = f32[128,128]{1,0:T(8,128)S(1)} custom-call(f32[128,128]{1,0:T(8,128)S(1)} %cholesky.599), custom_call_target="Cholesky" | custom-call | tf_op jit(solution)/shard_map/jit(cholesky)/cholesky | solution.py:49
  334.0 0.6 constant_dynamic-update-slice_fusion.2
  334.7 9.8 %custom-call.63 = f32[1,128,128]{1,2,0:T(8,128)S(1)} custom-call(f32[1,128,128]{2,1,0:T(8,128)S(1)} %get-tuple-element.10), custom_call_target="InvertDiagBlocksLowerTriangular" | custom-call | tf_op jit(solution)/shard_map/jit(cholesky)/cholesky | solution.py:49
  344.5 1.1 convolution_dynamic-update-slice_fusion.3
  345.6 3.1 convolution_subtract_fusion.4
  348.7 11.7 %cholesky.527 = f32[128,128]{1,0:T(8,128)S(1)} custom-call(f32[128,128]{1,0:T(8,128)S(1)} %cholesky.604), custom_call_target="Cholesky" | custom-call | tf_op jit(solution)/shard_map/jit(cholesky)/cholesky | solution.py:49
  360.6 0.6 constant_dynamic-update-slice_fusion.1
  361.2 9.8 %custom-call.64 = f32[1,128,128]{1,2,0:T(8,128)S(1)} custom-call(f32[1,128,128]{2,1,0:T(8,128)S(1)} %get-tuple-element.8), custom_call_target="InvertDiagBlocksLowerTriangular" | custom-call | tf_op jit(solution)/shard_map/jit(cholesky)/cholesky | solution.py:49
  371.0 1.0 convolution_dynamic-update-slice_fusion.4
  372.0 2.9 convolution_subtract_fusion.5
  374.9 11.7 %cholesky.547 = f32[128,128]{1,0:T(8,128)S(1)} custom-call(f32[128,128]{1,0:T(8,128)S(1)} %cholesky.609), custom_call_target="Cholesky" | custom-call | tf_op jit(solution)/shard_map/jit(cholesky)/cholesky | solution.py:49
  386.8 0.6 constant_dynamic-update-slice_fusion
  387.4 9.8 %custom-call.65 = f32[1,128,128]{1,2,0:T(8,128)S(1)} custom-call(f32[1,128,128]{2,1,0:T(8,128)S(1)} %get-tuple-element.6), custom_call_target="InvertDiagBlocksLowerTriangular" | custom-call | tf_op jit(solution)/shard_map/jit(cholesky)/cholesky | solution.py:49
  397.2 0.9 convolution_dynamic-update-slice_fusion.5
  398.2 2.1 convolution_subtract_fusion.6
  400.2 11.7 %cholesky.565 = f32[128,128]{1,0:T(8,128)S(1)} custom-call(f32[128,128]{1,0:T(8,128)S(1)} %convolution_subtract_fusion.6), custom_call_target="Cholesky" | custom-call | tf_op jit(solution)/shard_map/jit(cholesky)/cholesky | solution.py:49
  412.1 0.6 constant_dynamic-update-slice_fusion.4
  412.7 0.7 compare_reduce_fusion.5
  413.4 0.6 compare_reduce_fusion.4
  414.1 0.7 compare_reduce_fusion.3
  414.7 0.7 compare_reduce_fusion.2
  415.4 0.7 compare_reduce_fusion.1
  416.1 0.6 compare_reduce_fusion
  416.7 0.6 compare_reduce_fusion.6
  422.3 2.4 fusion.8
  (35 shorter events, 1.2 us)
Async XLA Ops:
  6.5 11.9 %copy-start = (f32[2,128,512]{2,1,0:T(8,128)S(1)}, f32[2,128,512]{2,1,0:T(8,128)}, u32[]{:S(2)}) copy-start(f32[2,128,512]{2,1,0:T(8,128)} %param.7) | copy-start | bytes 1572868
  11.1 7.3 %copy-start.3 = (s32[2,512]{1,0:T(2,128)S(1)}, s32[2,512]{1,0:T(2,128)}, u32[]{:S(2)}) copy-start(s32[2,512]{1,0:T(2,128)} %param.8) | copy-start | bytes 12292
  13.1 20.6 %all-to-all-start = ((f32[8,32,1024]{2,1,0:T(8,128)}), f32[8,32,1024]{2,1,0:T(8,128)S(1)}, u32[]{:S(2)}, u32[]{:S(2)}) async-start(f32[8,32,1024]{2,1,0:T(8,128)} %bitcast.5), calls=%async_computation | async-start | bytes 2097152 | tf_op jit(solution)/shard_map/all_to_all | solution.py:36
  18.3 178.4 %all-reduce.4.cloned.1.call-start = ((), (), s32[]{:S(2)}) async-start(), calls=%async_computation.1 | async-start | bytes 8388608 | tf_op jit(solution)/shard_map/psum | solution.py:47
  42.2 0.7 copy-start.2
  211.6 1.9 copy-start.1
Sparse Core Ops, SparseCore 0:
  42.3 154.3 all-reduce.3
where the time goes:
time: 438 us; the launch traced here: 432 us
  other arithmetic  182 us (42%)
  waiting for transfers between devices  168 us (38%)
  matrix products  37.1 us (8%)
  local copies, waits for them, and re-layouts  21 us (5%)
  between operations  19.5 us (4%)
  starting transfers between devices  5.24 us (1%)
    another operation x30, other arithmetic, local(): full_factor = jnp.linalg.cholesky(summed_gram).T  167 us
    psum x1, waiting for transfers between devices, local(): summed_gram = lax.psum(cross_product(stacked, stacked), 'sub')  154 us
    another operation x14, matrix products, local(): full_factor = jnp.linalg.cholesky(summed_gram).T  27 us
    all_to_all x1, waiting for transfers between devices, local(): lax.all_to_all(outgoing, 'front', split_axis=0, concat_axis=0, tiled=True)  13.7 us
    another operation x25, local copies, waits for them, and re-layouts, local(): full_factor = jnp.linalg.cholesky(summed_gram).T  8.78 us
  transfers between devices with their start and end apart: 2, of which 2 were waited for; matrix products, arithmetic and copies ran while one was open for 0% of the time, Pallas kernels for 0%

commit v1 on v0

--- a/solution.py
+++ b/solution.py
@@ -1,9 +1,139 @@
-import jax
-import jax.numpy as jnp
+import jax, jax.numpy as jnp
 from jax import lax
+from jax.experimental import pallas as pl
+from jax.experimental.pallas import tpu as pltpu
 from jax.sharding import PartitionSpec as P
 
 HIGHEST = lax.Precision.HIGHEST
+
+NB = 128
+BF = jnp.bfloat16
+F32 = jnp.float32
+
+
+def split3(x):
+    h = x.astype(BF)
+    r = x - h.astype(F32)
+    m = r.astype(BF)
+    l = (r - m.astype(F32)).astype(BF)
+    return h, m, l
+
+
+def split2(x):
+    h = x.astype(BF)
+    return h, (x - h.astype(F32)).astype(BF)
+
+
+def tdot(a, b):
+    return lax.dot_general(a, b, (((0,), (0,)), ((), ())), preferred_element_type=F32)
+
+
+def mm(a, b):
+    return lax.dot_general(a, b, (((1,), (0,)), ((), ())), preferred_element_type=F32)
+
+
+def factor_diag(m_ref, B):
+    for b in range(NB // B):
+        lo = b * B
+        rows = m_ref[lo:lo + B, :]
+        sub = lax.broadcasted_iota(jnp.int32, (B, 1), 0)
+        cs = [jnp.broadcast_to(rows[:, lo + j:lo + j + 1], (B, NB)) for j in range(B)]
+        for j in range(B):
+            c = cs[j]
+            r = lax.rsqrt(c[j:j + 1, :])
+            mult = jnp.where(sub > j, c * r, 0.0)
+            r2 = jnp.concatenate([r, r], axis=1)
+            pivot = rows[j:j + 1, :] * r2
+            m2 = jnp.concatenate([mult, mult], axis=1)
+            rows = jnp.where(sub == j, pivot, rows - m2 * pivot)
+            for i in range(j + 1, B):
+                cs[i] = cs[i] - mult * (cs[i][j:j + 1, :] * r)
+        m_ref[lo:lo + B, :] = rows
+        if lo + B < NB:
+            h, m, l = split3(rows)
+            left = jnp.concatenate([h, h, m, h, l, m], axis=0)[:, :NB]
+            right = jnp.concatenate([h, m, h, l, h, m], axis=0)
+            upd = tdot(left, right)
+            m_ref[lo + B:, :] = m_ref[lo + B:, :] - upd[lo + B:, :]
+
+
+def chol_body(own, per, B, g_ref, o_ref, a_ref, m_ref, rl_ref, rr_ref):
+    F = g_ref.shape[0]
+    panels = F // NB
+    a_ref[...] = g_ref[...]
+    ri = lax.broadcasted_iota(jnp.int32, (NB, NB), 0)
+    ci = lax.broadcasted_iota(jnp.int32, (NB, NB), 1)
+
+    def panel(p, carry):
+        p0 = pl.multiple_of(p * NB, NB)
+        m_ref[:, :NB] = a_ref[pl.ds(p0, NB), pl.ds(p0, NB)]
+        m_ref[:, NB:] = (ri == ci).astype(F32)
+        factor_diag(m_ref, B)
+        th, tl = split2(jnp.where(ci <= ri, m_ref[:, NB:], 0.0))
+        tcat = jnp.concatenate([th, th, tl], axis=1)
+
+        def cols(j, c):
+            j0 = pl.multiple_of(j * NB, NB)
+            h, l = split2(a_ref[pl.ds(p0, NB), pl.ds(j0, NB)])
+            r = mm(tcat, jnp.concatenate([h, l, h], axis=0))
+            a_ref[pl.ds(p0, NB), pl.ds(j0, NB)] = r
+            h, l = split2(r)
+            rl_ref[:, pl.ds(j0, NB)] = jnp.concatenate([h, h, l], axis=0)
+            rr_ref[:, pl.ds(j0, NB)] = jnp.concatenate([h, l, h], axis=0)
+            return c
+
+        lax.fori_loop(p + 1, panels, cols, 0)
+        a_ref[pl.ds(p0, NB), pl.ds(p0, NB)] = jnp.where(ci >= ri, m_ref[:, :NB], 0.0)
+
+        @pl.when(p // per == own)
+        def _():
+            off = pl.multiple_of((p - own * per) * NB, NB)
+            def put(j, c):
+                j0 = pl.multiple_of(j * NB, NB)
+                v = a_ref[pl.ds(p0, NB), pl.ds(j0, NB)]
+                o_ref[pl.ds(off, NB), pl.ds(j0, NB)] = jnp.where(j >= p, v, 0.0)
+                return c
+            lax.fori_loop(0, panels, put, 0)
+
+        def trail(i, c):
+            i0 = pl.multiple_of(i * NB, NB)
+            lt = rl_ref[:, pl.ds(i0, NB)].T
+
+            def inner(j, cc):
+                j0 = pl.multiple_of(j * NB, NB)
+                a_ref[pl.ds(i0, NB), pl.ds(j0, NB)] -= mm(lt, rr_ref[:, pl.ds(j0, NB)])
+                return cc
+
+            lax.fori_loop(i, panels, inner, 0)
+            return c
+
+        lax.fori_loop(p + 1, panels, trail, 0)
+        return carry
+
+    lax.fori_loop(0, (own + 1) * per, panel, 0)
+
+
+def chol(g, subs, B=16):
+    F = g.shape[0]
+    rows = F // subs
+
+    def body(g_ref, o_ref, *scratch):
+        chol_body(lax.axis_index("sub"), rows // NB, B, g_ref, o_ref, *scratch)
+
+    return pl.pallas_call(
+        body,
+        out_shape=jax.ShapeDtypeStruct((rows, F), F32),
+        in_specs=[pl.BlockSpec(memory_space=pltpu.VMEM)],
+        out_specs=pl.BlockSpec(memory_space=pltpu.VMEM),
+        scratch_shapes=[
+            pltpu.VMEM((F, F), F32),
+            pltpu.VMEM((NB, 2 * NB), F32),
+            pltpu.VMEM((3 * NB, F), BF),
+            pltpu.VMEM((3 * NB, F), BF),
+        ],
+        compiler_params=pltpu.CompilerParams(vmem_limit_bytes=40 << 20),
+        name="chol",
+    )(g)
 
 
 def cross_product(left_cols, right_cols):
@@ -41,14 +171,10 @@
     )
     stacked = jnp.concatenate([placed.reshape(-1, front_width), received], axis=0)
     sub_count = lax.axis_size("sub")
-    block_rows = front_width // sub_count
-    own_index = lax.axis_index("sub")
     weight = damping[0]
     summed_gram = lax.psum(cross_product(stacked, stacked), "sub")
     summed_gram = summed_gram + jnp.diag(weight * weight)
-    full_factor = jnp.linalg.cholesky(summed_gram).T
-    own_rows = lax.dynamic_slice_in_dim(full_factor, own_index * block_rows, block_rows, 0)
-    return own_rows[None]
+    return chol(summed_gram, sub_count)[None]
 
 
 def solution(mesh):

time: 438 us -> 255 us (0.58)
  the two profiles are of different devices: /device:TPU:0 before, /device:TPU:27 now
where the time goes in v1:
time: 255 us; the launch traced here: 254 us
  waiting for transfers between devices  165 us (65%)
  Pallas kernels  51.6 us (20%)
  between operations  13.5 us (5%)
  matrix products  9.95 us (4%)
  other arithmetic  5.31 us (2%)
  local copies, waits for them, and re-layouts  4.75 us (2%)
  starting transfers between devices  4.54 us (2%)
    psum x1, waiting for transfers between devices, local(): summed_gram = lax.psum(cross_product(stacked, stacked), 'sub')  152 us
    pallas_call x1, Pallas kernels, chol(): pl.pallas_call(body, out_shape=jax.ShapeDtypeStruct((rows, F), F32), in_s...  51.6 us
    all_to_all x1, waiting for transfers between devices, local(): lax.all_to_all(outgoing, 'front', split_axis=0, concat_axis=0, tiled=True)  12.2 us
    dot_general x1, matrix products, cross_product(): lax.dot_general(left_cols, right_cols, (((0,), (0,)), ((), ())), precisio...  8.34 us
  transfers between devices with their start and end apart: 2, of which 2 were waited for; matrix products, arithmetic and copies ran while one was open for 1% of the time, Pallas kernels for 0%

profile of v1, /device:TPU:27, one launch (start us, length us, event | category | flops | bytes accessed | tf_op | source)
XLA Modules:
  0.0 254.3 jit_solution(14966984993219170462)
XLA Ops:
  6.5 0.0 copy-start
  6.5 0.8 fusion.6
  7.3 0.2 reduce_window_sum.11
  7.5 0.8 select_reduce_fusion
  8.3 0.7 fusion.7
  9.0 1.0 scatter_custom_fusion
  10.0 1.1 concatenate.6
  11.1 0.0 copy-start.2
  11.1 2.0 gather_fusion
  13.1 4.5 %all-to-all-start = ((f32[8,32,1024]{2,1,0:T(8,128)}), f32[8,32,1024]{2,1,0:T(8,128)S(1)}, u32[]{:S(2)}, u32[]{:S(2)}) async-start(f32[8,32,1024]{2,1,0:T(8,128)} %bitcast.5), calls=%async_computation | async-start | bytes 2097152 | tf_op jit(solution)/shard_map/all_to_all | solution.py:166
  17.7 0.0 all-reduce.3.cloned.1.call-start
  17.7 0.0 copy-done
  17.7 0.0 copy-done.2
  17.7 1.6 fusion
  19.3 12.2 %all-to-all-done = f32[8,32,1024]{2,1,0:T(8,128)S(1)} async-done(((f32[8,32,1024]{2,1,0:T(8,128)}), f32[8,32,1024]{2,1,0:T(8,128)S(1)}, u32[]{:S(2)}, u32[]{:S(2)}) %all-to-all-start) | async-done | bytes 1048608 | tf_op jit(solution)/shard_map/all_to_all | solution.py:166
  31.5 8.3 %fusion.1 = f32[1024,1024]{1,0:T(8,128)} fusion(f32[256,1024]{1,0:T(8,128)S(1)} %bitcast.15, f32[256,1024]{1,0:T(8,128)S(1)} %bitcast.19), kind=kOutput, calls=%fused_computation.6 | convolution fusion | flops 6442975232 | bytes 6291456 | tf_op jit(solution)/shard_map/dot_general | solution.py:140
  39.8 0.0 copy-start.1
  39.8 0.0 all-reduce.3.cloned.1.call-update
  39.9 0.7 copy-done.1
  40.5 152.4 %all-reduce.3.cloned.1.call-done = f32[1024,1024]{1,0:T(8,128)} async-done(((f32[1024,1024]{1,0:T(8,128)}), f32[1024,1024]{1,0:T(8,128)}) %all-reduce.3.cloned.1.call-update) | async-done | bytes 4194320 | tf_op jit(solution)/shard_map/psum | solution.py:175
  193.0 2.8 %select_add_fusion.g_ref = f32[1024,1024]{1,0:T(8,128)S(1)} fusion(f32[1024,1024]{1,0:T(8,128)} %all-reduce.3.cloned.1.call-done, f32[1024]{0:T(1024)S(1)} %bitcast.16), kind=kLoop, calls=%fused_computation.2 | loop fusion | flops 3145728 | bytes 8392704 | tf_op jit(solution)/shard_map/add | solution.py:176
  195.8 51.6 %chol.1 = f32[256,1024]{1,0:T(8,128)} custom-call(f32[1024,1024]{1,0:T(8,128)S(1)} %select_add_fusion.g_ref), custom_call_target="tpu_custom_call" | custom-call | tf_op jit(solution)/shard_map/chol/pallas_call | solution.py:123
  (4 shorter events, 0.0 us)
Async XLA Ops:
  6.5 11.1 %copy-start = (f32[2,128,512]{2,1,0:T(8,128)S(1)}, f32[2,128,512]{2,1,0:T(8,128)}, u32[]{:S(2)}) copy-start(f32[2,128,512]{2,1,0:T(8,128)} %param.7) | copy-start | bytes 1572868
  11.1 6.6 %copy-start.2 = (s32[2,512]{1,0:T(2,128)S(1)}, s32[2,512]{1,0:T(2,128)}, u32[]{:S(2)}) copy-start(s32[2,512]{1,0:T(2,128)} %param.8) | copy-start | bytes 12292
  13.1 18.4 %all-to-all-start = ((f32[8,32,1024]{2,1,0:T(8,128)}), f32[8,32,1024]{2,1,0:T(8,128)S(1)}, u32[]{:S(2)}, u32[]{:S(2)}) async-start(f32[8,32,1024]{2,1,0:T(8,128)} %bitcast.5), calls=%async_computation | async-start | bytes 2097152 | tf_op jit(solution)/shard_map/all_to_all | solution.py:166
  17.7 175.3 %all-reduce.3.cloned.1.call-start = ((), (), s32[]{:S(2)}) async-start(), calls=%async_computation.1 | async-start | bytes 8388608 | tf_op jit(solution)/shard_map/psum | solution.py:175
  39.8 0.7 copy-start.1
Sparse Core Ops, SparseCore 0:
  40.0 152.9 all-reduce.2

commit v2 on v1

v2 whole, which is shorter than its diff:
```python
import functools
import jax, jax.numpy as jnp
from jax import lax
from jax.experimental import pallas as pl
from jax.experimental.pallas import tpu as pltpu
from jax.sharding import PartitionSpec as P

HIGHEST = lax.Precision.HIGHEST

NB = 128
LAG = 3
BF = jnp.bfloat16
F32 = jnp.float32


def split3(x):
    h = x.astype(BF)
    r = x - h.astype(F32)
    m = r.astype(BF)
    l = (r - m.astype(F32)).astype(BF)
    return h, m, l


def split2(x):
    h = x.astype(BF)
    return h, (x - h.astype(F32)).astype(BF)


def tdot(a, b):
    return lax.dot_general(a, b, (((0,), (0,)), ((), ())), preferred_element_type=F32)


def mm(a, b):
    return lax.dot_general(a, b, (((1,), (0,)), ((), ())), preferred_element_type=F32)


def factor_diag(m_ref, B, slot):
    for b in range(NB // B):
        lo = b * B
        slot(b)
        rows = m_ref[lo:lo + B, :]
        sub = lax.broadcasted_iota(jnp.int32, (B, 1), 0)
        cs = [jnp.broadcast_to(rows[:, lo + j:lo + j + 1], (B, NB)) for j in range(B)]
        for j in range(B):
            c = cs[j]
            r = lax.rsqrt(c[j:j + 1, :])
            mult = jnp.where(sub > j, c * r, 0.0)
            r2 = jnp.concatenate([r, r], axis=1)
            pivot = rows[j:j + 1, :] * r2
            m2 = jnp.concatenate([mult, mult], axis=1)
            rows = jnp.where(sub == j, pivot, rows - m2 * pivot)
            for i in range(j + 1, B):
                cs[i] = cs[i] - mult * (cs[i][j:j + 1, :] * r)
        m_ref[lo:lo + B, :] = rows
        if lo + B < NB:
            h, m, l = split3(rows)
            left = jnp.concatenate([h, h, m, h, l, m], axis=0)[:, :NB]
            right = jnp.concatenate([h, m, h, l, h, m], axis=0)
            upd = tdot(left, right)
            m_ref[lo + B:, :] = m_ref[lo + B:, :] - upd[lo + B:, :]


MESH = pl.DeviceIdType.MESH


def fused_body(n, B, x_ref, w_ref, o_ref, a_ref, m_ref, rl_ref, rr_ref, xl_ref, xr_ref, p_ref, l_ref, r_ref, fr_ref, fl_ref, sr, sl, gl, gr):
    K, F = x_ref.shape
    panels = F // NB
    per = panels // n
    me = lax.axis_index("sub")
    right, left = lax.rem(me + 1, n), lax.rem(me + n - 1, n)
    first, last = me == 0, me == n - 1

    barrier = pltpu.get_barrier_semaphore()
    for peer in (left, right):
        pl.semaphore_signal(barrier, inc=1, device_id={"sub": peer}, device_id_type=MESH)
    pl.semaphore_wait(barrier, 2)

    ri = lax.broadcasted_iota(jnp.int32, (NB, NB), 0)
    ci = lax.broadcasted_iota(jnp.int32, (NB, NB), 1)

    def at(i, j):
        return (pl.ds(pl.multiple_of(i * NB, NB), NB), pl.ds(pl.multiple_of(j * NB, NB), NB))

    total = panels * (panels + 1) // 2
    ahead_left, ahead_right = LAG * (n - 1 - me), LAG * me

    def place(i, j):
        return i * panels - i * (i - 1) // 2 + j - i

    def to_right(src, c):
        return pltpu.make_async_remote_copy(
            src_ref=src.at[c], dst_ref=l_ref.at[c], send_sem=sr.at[c], recv_sem=gl.at[c],
            device_id={"sub": right}, device_id_type=MESH)

    def to_left(src, c):
        return pltpu.make_async_remote_copy(
            src_ref=src.at[c], dst_ref=r_ref.at[c], send_sem=sl.at[c], recv_sem=gr.at[c],
            device_id={"sub": left}, device_id_type=MESH)

    h, l = split2(x_ref[...])
    xr_ref[...] = jnp.concatenate([h, l, h], axis=0)
    xl_ref[...] = jnp.concatenate([h, h, l], axis=0)

    def gram_row(i, carry):
        lt = xl_ref[:, pl.ds(pl.multiple_of(i * NB, NB), NB)].T

        def gram_col(j, c):
            c0 = place(i, j)
            p_ref[c0] = mm(lt, xr_ref[:, pl.ds(pl.multiple_of(j * NB, NB), NB)])

            @pl.when(first)
            def _():
                to_right(p_ref, c0).start()

            @pl.when(last)
            def _():
                to_left(p_ref, c0).start()
            return c

        return lax.fori_loop(i, panels, gram_col, carry)

    lax.fori_loop(0, panels, gram_row, 0)

    def from_left(c):
        @pl.when((me > 0) & (c >= 0) & (c < total))
        def _():
            to_right(fr_ref, c).wait_recv()

            @pl.when(me < n - 1)
            def _():
                fr_ref[c] = l_ref[c] + p_ref[c]
                to_right(fr_ref, c).start()

    def from_right(c):
        @pl.when((me < n - 1) & (c >= 0) & (c < total))
        def _():
            to_left(fl_ref, c).wait_recv()

            @pl.when(me > 0)
            def _():
                fl_ref[c] = r_ref[c] + p_ref[c]
                to_left(fl_ref, c).start()

    def pass_on(q):
        from_left(q + ahead_left)
        from_right(q + ahead_right)

    def serve(i, j):
        c = place(i, j)
        pass_on(c)

        @pl.when(first)
        def _():
            a_ref[at(i, j)] = p_ref[c] + r_ref[c]

        @pl.when(last)
        def _():
            a_ref[at(i, j)] = p_ref[c] + l_ref[c]

        @pl.when((me > 0) & (me < n - 1))
        def _():
            a_ref[at(i, j)] = fr_ref[c] + r_ref[c]

        @pl.when(i == j)
        def _():
            wt = w_ref[:, pl.ds(pl.multiple_of(i * NB, NB), NB)]
            a_ref[at(i, j)] += jnp.where(ri == ci, wt * wt, 0.0)

    def fill(t, c):
        pass_on(t - LAG * (n - 1))
        return c

    lax.fori_loop(0, LAG * (n - 1), fill, 0)

    def first_row(j, c):
        serve(0, j)
        return c

    lax.fori_loop(0, panels, first_row, 0)

    def panel(p, carry):
        m_ref[:, :NB] = a_ref[at(p, p)]
        m_ref[:, NB:] = (ri == ci).astype(F32)

        def slot(k):
            @pl.when(p + 1 + k < panels)
            def _():
                serve(p + 1, p + 1 + k)

        factor_diag(m_ref, B, slot)

        def rest(k, c):
            @pl.when(p + 1 + k < panels)
            def _():
                serve(p + 1, p + 1 + k)
            return c

        lax.fori_loop(NB // B, max(NB // B, panels - 1), rest, 0)
        th, tl = split2(jnp.where(ci <= ri, m_ref[:, NB:], 0.0))
        tcat = jnp.concatenate([th, th, tl], axis=1)

        def cols(j, c):
            j0 = pl.multiple_of(j * NB, NB)
            h, l = split2(a_ref[at(p, j)])
            r = mm(tcat, jnp.concatenate([h, l, h], axis=0))
            a_ref[at(p, j)] = r
            h, l = split2(r)
            rl_ref[p, :, pl.ds(j0, NB)] = jnp.concatenate([h, h, l], axis=0)
            rr_ref[p, :, pl.ds(j0, NB)] = jnp.concatenate([h, l, h], axis=0)
            return c

        lax.fori_loop(p + 1, panels, cols, 0)
        a_ref[at(p, p)] = jnp.where(ci >= ri, m_ref[:, :NB], 0.0)

        @pl.when(p // per == me)
        def _():
            off = p - me * per

            def put(j, c):
                o_ref[at(off, j)] = jnp.where(j >= p, a_ref[at(p, j)], 0.0)
                return c
            lax.fori_loop(0, panels, put, 0)

        @pl.when(p + 1 < panels)
        def _():
            def term(q, c):
                lt = rl_ref[q, :, pl.ds(pl.multiple_of((p + 1) * NB, NB), NB)].T

                def inner(j, cc):
                    a_ref[at(p + 1, j)] -= mm(lt, rr_ref[q, :, pl.ds(pl.multiple_of(j * NB, NB), NB)])
                    return cc
                return lax.fori_loop(p + 1, panels, inner, c)
            lax.fori_loop(0, p + 1, term, 0)
        return carry

    lax.fori_loop(0, panels, panel, 0)

    def drain(c, carry):
        @pl.when(me < n - 1)
        def _():
            to_right(fr_ref, c).wait_send()

        @pl.when(me > 0)
        def _():
            to_left(fl_ref, c).wait_send()
        return carry

    lax.fori_loop(0, total, drain, 0)


def merge(x, w, n, B=16):
    K, F = x.shape
    panels = F // NB
    total = panels * (panels + 1) // 2
    sems = pltpu.SemaphoreType.DMA((total,))
    return pl.pallas_call(
        functools.partial(fused_body, n, B),
        out_shape=jax.ShapeDtypeStruct((F // n, F), F32),
        in_specs=[pl.BlockSpec(memory_space=pltpu.VMEM)] * 2,
        out_specs=pl.BlockSpec(memory_space=pltpu.VMEM),
        scratch_shapes=[
            pltpu.VMEM((F, F), F32),
            pltpu.VMEM((NB, 2 * NB), F32),
            pltpu.VMEM((panels, 3 * NB, F), BF),
            pltpu.VMEM((panels, 3 * NB, F), BF),
            pltpu.VMEM((3 * K, F), BF),
            pltpu.VMEM((3 * K, F), BF),
        ] + [pltpu.VMEM((total, NB, NB), F32)] * 5 + [sems] * 4,
        compiler_params=pltpu.CompilerParams(
            vmem_limit_bytes=60 << 20, collective_id=0, has_side_effects=True),
        name="merge",
    )(x, w)


def local(row_values, front_of_row, child_factors, child_columns, damping):
    fronts = lax.axis_size("front")
    rows_held, front_width = row_values.shape
    capacity = 2 * rows_held // fronts
    destination = front_of_row[:, 0]
    onehot = (destination[:, None] == jnp.arange(fronts, dtype=jnp.int32)[None, :]).astype(
        jnp.int32
    )
    position = jnp.sum((jnp.cumsum(onehot, axis=0) - onehot) * onehot, axis=1)
    slot_of = destination * capacity + position
    source = (
        jnp.full((fronts * capacity,), rows_held, jnp.int32)
        .at[slot_of]
        .set(jnp.arange(rows_held, dtype=jnp.int32))
    )
    padded = jnp.concatenate([row_values, jnp.zeros((1, front_width), row_values.dtype)], axis=0)
    outgoing = padded[source]
    received = lax.all_to_all(outgoing, "front", split_axis=0, concat_axis=0, tiled=True)
    columns = jnp.arange(front_width, dtype=jnp.int32)
    spread = (child_columns[:, :, None] == columns[None, None, :]).astype(jnp.float32)
    placed = jnp.einsum(
        "jrc,jcf->jrf", child_factors, spread, precision=HIGHEST, preferred_element_type=jnp.float32
    )
    stacked = jnp.concatenate([placed.reshape(-1, front_width), received], axis=0)
    sub_count = lax.axis_size("sub")
    return merge(stacked, damping, sub_count)[None]


def solution(mesh):
    in_specs = (
        P(("front", "sub"), None),
        P(("front", "sub"), None),
        P("front", "sub", None),
        P("front", None),
        P("front", None),
    )
    out_specs = P("front", "sub", None)
    return jax.shard_map(local, mesh=mesh, in_specs=in_specs, out_specs=out_specs, check_vma=False)
```

time: 255 us -> 133 us (0.52)
  the two profiles are of different devices: /device:TPU:27 before, /device:TPU:0 now
where the time goes in v2:
time: 133 us; the launch traced here: 132 us
  Pallas kernels  101 us (76%)
  waiting for transfers between devices  13.7 us (10%)
  local copies, waits for them, and re-layouts  6.39 us (5%)
  starting transfers between devices  5.33 us (4%)
  other arithmetic  3.96 us (3%)
  matrix products  1.6 us (1%)
    pallas_call x1, Pallas kernels, merge(): pl.pallas_call(functools.partial(fused_body, n, B), out_shape=jax.ShapeDt...  101 us
    all_to_all x1, waiting for transfers between devices, local(): lax.all_to_all(outgoing, 'front', split_axis=0, concat_axis=0, tiled=True)  13.7 us
    all_to_all x1, starting transfers between devices, local(): lax.all_to_all(outgoing, 'front', split_axis=0, concat_axis=0, tiled=True)  5.33 us
  transfers between devices with their start and end apart: 1, of which 1 were waited for; matrix products, arithmetic and copies ran while one was open for 1% of the time, Pallas kernels for 0%

profile of v2, /device:TPU:0, one launch (start us, length us, event | category | flops | bytes accessed | tf_op | source)
XLA Modules:
  0.0 132.5 jit_solution(9896064543604680618)
XLA Ops:
  0.0 0.0 copy-start
  0.0 0.8 fusion.2
  0.8 0.2 reduce_window_sum.11
  1.0 0.8 select_reduce_fusion
  1.8 0.7 fusion.3
  2.5 1.0 scatter_custom_fusion
  3.5 1.1 concatenate.6
  4.6 2.0 %gather_fusion = f32[256,1024]{1,0:T(8,128)} fusion(f32[129,1024]{1,0:T(8,128)S(1)} %concatenate.6, s32[1024]{0:T(1024)S(1)} %pad_clamp_fusion), kind=kCustom, calls=%fused_computation | custom fusion | bytes 2098176 | tf_op jit(solution)/shard_map/gather | solution.py:292
  6.6 0.0 copy-start.1
  6.6 5.3 %all-to-all-start = ((f32[8,32,1024]{2,1,0:T(8,128)}), f32[8,32,1024]{2,1,0:T(8,128)S(1)}, u32[]{:S(2)}, u32[]{:S(2)}) async-start(f32[8,32,1024]{2,1,0:T(8,128)} %bitcast.5), calls=%async_computation | async-start | bytes 2097152 | tf_op jit(solution)/shard_map/all_to_all | solution.py:293
  11.9 0.0 copy-done
  11.9 0.0 copy-done.1
  11.9 1.6 %fusion = f32[2,1024,128]{1,2,0:T(8,128)S(1)} fusion(f32[2,128,512]{2,1,0:T(8,128)S(1)} %copy-done, s32[2,512]{1,0:T(2,128)S(1)} %copy-done.1), kind=kOutput, calls=%fused_computation.3 | convolution fusion | flops 1611661312 | bytes 1576960 | tf_op jit(solution)/shard_map/jrc,jcf->jrf/dot_general | solution.py:296
  13.6 13.7 %all-to-all-done = f32[8,32,1024]{2,1,0:T(8,128)S(1)} async-done(((f32[8,32,1024]{2,1,0:T(8,128)}), f32[8,32,1024]{2,1,0:T(8,128)S(1)}, u32[]{:S(2)}, u32[]{:S(2)}) %all-to-all-start) | async-done | bytes 1048608 | tf_op jit(solution)/shard_map/all_to_all | solution.py:293
  27.3 1.5 %pad_maximum_fusion.x_ref = f32[512,1024]{1,0:T(8,128)} fusion(f32[256,1024]{1,0:T(8,128)S(1)} %bitcast.16, f32[256,1024]{1,0:T(8,128)S(1)} %bitcast.17), kind=kLoop, calls=%fused_computation.4 | loop fusion | flops 524288 | bytes 4194304 | tf_op jit(solution)/shard_map/concatenate | solution.py:299
  28.8 101.4 %merge.1 = f32[256,1024]{1,0:T(8,128)} custom-call(f32[512,1024]{1,0:T(8,128)} %pad_maximum_fusion.x_ref, f32[1,1024]{1,0:T(1,128)} %w_ref.1), custom_call_target="tpu_custom_call" | custom-call | tf_op jit(solution)/shard_map/merge/pallas_call | solution.py:257
  130.2 2.3 %copy.7 = f32[1,256,1024]{2,1,0:T(8,128)} copy(f32[1,256,1024]{2,1,0:T(8,128)} %bitcast.15) | data formatting | bytes 2097152
  (3 shorter events, 0.0 us)
Async XLA Ops:
  0.0 11.9 %copy-start = (f32[2,128,512]{2,1,0:T(8,128)S(1)}, f32[2,128,512]{2,1,0:T(8,128)}, u32[]{:S(2)}) copy-start(f32[2,128,512]{2,1,0:T(8,128)} %param.7) | copy-start | bytes 1572868
  6.6 5.3 %copy-start.1 = (s32[2,512]{1,0:T(2,128)S(1)}, s32[2,512]{1,0:T(2,128)}, u32[]{:S(2)}) copy-start(s32[2,512]{1,0:T(2,128)} %param.8) | copy-start | bytes 12292
  6.6 20.7 %all-to-all-start = ((f32[8,32,1024]{2,1,0:T(8,128)}), f32[8,32,1024]{2,1,0:T(8,128)S(1)}, u32[]{:S(2)}, u32[]{:S(2)}) async-start(f32[8,32,1024]{2,1,0:T(8,128)} %bitcast.5), calls=%async_computation | async-start | bytes 2097152 | tf_op jit(solution)/shard_map/all_to_all | solution.py:293

commit v3 on v2

--- a/solution.py
+++ b/solution.py
@@ -4,8 +4,6 @@
 from jax.experimental import pallas as pl
 from jax.experimental.pallas import tpu as pltpu
 from jax.sharding import PartitionSpec as P
-
-HIGHEST = lax.Precision.HIGHEST
 
 NB = 128
 LAG = 3
@@ -63,18 +61,72 @@
 MESH = pl.DeviceIdType.MESH
 
 
-def fused_body(n, B, x_ref, w_ref, o_ref, a_ref, m_ref, rl_ref, rr_ref, xl_ref, xr_ref, p_ref, l_ref, r_ref, fr_ref, fl_ref, sr, sl, gl, gr):
-    K, F = x_ref.shape
+def fused_body(n, fronts, cap, B, x_ref, d_ref, ch_ref, cc_ref, w_ref, o_ref, out_ref, in_ref, fs, fg, a_ref, m_ref, rl_ref, rr_ref, xl_ref, xr_ref, p_ref, l_ref, r_ref, fr_ref, fl_ref, sr, sl, gl, gr):
+    R, F = x_ref.shape
+    kids, crows, _ = ch_ref.shape
+    slots = fronts * cap
+    K = kids * crows + slots
     panels = F // NB
     per = panels // n
     me = lax.axis_index("sub")
     right, left = lax.rem(me + 1, n), lax.rem(me + n - 1, n)
     first, last = me == 0, me == n - 1
 
+    mine = lax.axis_index("front")
     barrier = pltpu.get_barrier_semaphore()
     for peer in (left, right):
         pl.semaphore_signal(barrier, inc=1, device_id={"sub": peer}, device_id_type=MESH)
-    pl.semaphore_wait(barrier, 2)
+
+    def greet(k, c):
+        pl.semaphore_signal(barrier, inc=1, device_id={"front": lax.rem(mine + k, fronts)}, device_id_type=MESH)
+        return c
+
+    lax.fori_loop(1, fronts, greet, 0)
+
+    dest = d_ref[...]
+    hot = dest == lax.broadcasted_iota(jnp.int32, (R, fronts), 1)
+    below = lax.broadcasted_iota(jnp.int32, (R, R), 1) < lax.broadcasted_iota(jnp.int32, (R, R), 0)
+    before = mm(below.astype(F32).astype(BF), hot.astype(F32).astype(BF))
+    position = jnp.sum(jnp.where(hot, before, 0.0), axis=1, keepdims=True)
+    slot_of = dest.astype(F32) * cap + position
+    pick = (slot_of == lax.broadcasted_iota(jnp.int32, (R, slots), 1).astype(F32)).astype(F32).astype(BF)
+    out_ref[...] = tdot(jnp.concatenate([pick] * 3, axis=0), jnp.concatenate(split3(x_ref[...]), axis=0))
+    pl.semaphore_wait(barrier, fronts + 1)
+
+    def rows_of(f):
+        return pl.ds(pl.multiple_of(f * cap, cap), cap)
+
+    def post(k, dst_front):
+        to = lax.rem(mine + k, fronts)
+        return pltpu.make_async_remote_copy(
+            src_ref=out_ref.at[rows_of(to)], dst_ref=in_ref.at[rows_of(dst_front)], send_sem=fs.at[k],
+            recv_sem=fg.at[k], device_id={"front": to}, device_id_type=MESH)
+
+    def post_rows(k, c):
+        post(k, mine).start()
+        return c
+
+    lax.fori_loop(1, fronts, post_rows, 0)
+    in_ref[rows_of(mine), :] = out_ref[rows_of(mine), :]
+
+    def keep(start, count, h, l):
+        for ref, parts in ((xr_ref, (h, l, h)), (xl_ref, (h, h, l))):
+            for t, part in enumerate(parts):
+                ref[t * K + start:t * K + start + count, :] = part
+
+    for kid in range(kids):
+        h, l = split2(ch_ref[kid])
+        spread = (lax.broadcasted_iota(jnp.int32, (F, cc_ref.shape[1]), 0) == cc_ref[kid:kid + 1, :]).astype(F32).astype(BF)
+        both = lax.dot_general(jnp.concatenate([h, l], axis=0), spread, (((1,), (1,)), ((), ())), preferred_element_type=F32)
+        keep(kid * crows, crows, both[:crows].astype(BF), both[crows:].astype(BF))
+
+    def take(k, c):
+        post(k, lax.rem(mine + fronts - k, fronts)).wait_recv()
+        return c
+
+    lax.fori_loop(1, fronts, take, 0)
+    h, l = split2(in_ref[...])
+    keep(kids * crows, slots, h, l)
 
     ri = lax.broadcasted_iota(jnp.int32, (NB, NB), 0)
     ci = lax.broadcasted_iota(jnp.int32, (NB, NB), 1)
@@ -98,29 +150,37 @@
             src_ref=src.at[c], dst_ref=r_ref.at[c], send_sem=sl.at[c], recv_sem=gr.at[c],
             device_id={"sub": left}, device_id_type=MESH)
 
-    h, l = split2(x_ref[...])
-    xr_ref[...] = jnp.concatenate([h, l, h], axis=0)
-    xl_ref[...] = jnp.concatenate([h, h, l], axis=0)
+    WB = 2 * NB
 
     def gram_row(i, carry):
-        lt = xl_ref[:, pl.ds(pl.multiple_of(i * NB, NB), NB)].T
+        lt = xl_ref[:, pl.ds(pl.multiple_of(i * WB, WB), WB)].T
 
         def gram_col(j, c):
-            c0 = place(i, j)
-            p_ref[c0] = mm(lt, xr_ref[:, pl.ds(pl.multiple_of(j * NB, NB), NB)])
-
+            block = mm(lt, xr_ref[:, pl.ds(pl.multiple_of(j * WB, WB), WB)])
+            p_ref[place(2 * i, 2 * j)] = block[:NB, :NB]
+            p_ref[place(2 * i, 2 * j + 1)] = block[:NB, NB:]
+            p_ref[place(2 * i + 1, 2 * j + 1)] = block[NB:, NB:]
+
+            @pl.when(j > i)
+            def _():
+                p_ref[place(2 * i + 1, 2 * j)] = block[NB:, :NB]
+            return c
+
+        lax.fori_loop(i, panels // 2, gram_col, 0)
+
+        def launch(c, cc):
             @pl.when(first)
             def _():
-                to_right(p_ref, c0).start()
+                to_right(p_ref, c).start()
 
             @pl.when(last)
             def _():
-                to_left(p_ref, c0).start()
-            return c
-
-        return lax.fori_loop(i, panels, gram_col, carry)
-
-    lax.fori_loop(0, panels, gram_row, 0)
+                to_left(p_ref, c).start()
+            return cc
+
+        return lax.fori_loop(place(2 * i, 2 * i), place(2 * i + 2, 2 * i + 2), launch, carry)
+
+    lax.fori_loop(0, panels // 2, gram_row, 0)
 
     def from_left(c):
         @pl.when((me > 0) & (c >= 0) & (c < total))
@@ -248,18 +308,31 @@
 
     lax.fori_loop(0, total, drain, 0)
 
-
-def merge(x, w, n, B=16):
-    K, F = x.shape
+    def sent(k, c):
+        post(k, mine).wait_send()
+        return c
+
+    lax.fori_loop(1, fronts, sent, 0)
+
+
+def local(row_values, front_of_row, child_factors, child_columns, damping, B=16):
+    fronts, n = lax.axis_size("front"), lax.axis_size("sub")
+    rows_held, F = row_values.shape
+    cap = -(-(2 * rows_held // fronts) // 8) * 8
+    K = fronts * cap + child_factors.shape[0] * child_factors.shape[1]
     panels = F // NB
     total = panels * (panels + 1) // 2
     sems = pltpu.SemaphoreType.DMA((total,))
     return pl.pallas_call(
-        functools.partial(fused_body, n, B),
+        functools.partial(fused_body, n, fronts, cap, B),
         out_shape=jax.ShapeDtypeStruct((F // n, F), F32),
-        in_specs=[pl.BlockSpec(memory_space=pltpu.VMEM)] * 2,
+        in_specs=[pl.BlockSpec(memory_space=pltpu.VMEM)] * 5,
         out_specs=pl.BlockSpec(memory_space=pltpu.VMEM),
         scratch_shapes=[
+            pltpu.VMEM((fronts * cap, F), F32),
+            pltpu.VMEM((fronts * cap, F), F32),
+            pltpu.SemaphoreType.DMA((fronts,)),
+            pltpu.SemaphoreType.DMA((fronts,)),
             pltpu.VMEM((F, F), F32),
             pltpu.VMEM((NB, 2 * NB), F32),
             pltpu.VMEM((panels, 3 * NB, F), BF),
@@ -270,35 +343,7 @@
         compiler_params=pltpu.CompilerParams(
             vmem_limit_bytes=60 << 20, collective_id=0, has_side_effects=True),
         name="merge",
-    )(x, w)
-
-
-def local(row_values, front_of_row, child_factors, child_columns, damping):
-    fronts = lax.axis_size("front")
-    rows_held, front_width = row_values.shape
-    capacity = 2 * rows_held // fronts
-    destination = front_of_row[:, 0]
-    onehot = (destination[:, None] == jnp.arange(fronts, dtype=jnp.int32)[None, :]).astype(
-        jnp.int32
-    )
-    position = jnp.sum((jnp.cumsum(onehot, axis=0) - onehot) * onehot, axis=1)
-    slot_of = destination * capacity + position
-    source = (
-        jnp.full((fronts * capacity,), rows_held, jnp.int32)
-        .at[slot_of]
-        .set(jnp.arange(rows_held, dtype=jnp.int32))
-    )
-    padded = jnp.concatenate([row_values, jnp.zeros((1, front_width), row_values.dtype)], axis=0)
-    outgoing = padded[source]
-    received = lax.all_to_all(outgoing, "front", split_axis=0, concat_axis=0, tiled=True)
-    columns = jnp.arange(front_width, dtype=jnp.int32)
-    spread = (child_columns[:, :, None] == columns[None, None, :]).astype(jnp.float32)
-    placed = jnp.einsum(
-        "jrc,jcf->jrf", child_factors, spread, precision=HIGHEST, preferred_element_type=jnp.float32
-    )
-    stacked = jnp.concatenate([placed.reshape(-1, front_width), received], axis=0)
-    sub_count = lax.axis_size("sub")
-    return merge(stacked, damping, sub_count)[None]
+    )(row_values, front_of_row, child_factors, child_columns, damping)[None]
 
 
 def solution(mesh):

time: 133 us -> 117 us (0.88)
  the two profiles are of different devices: /device:TPU:0 before, /device:TPU:1 now
where the time goes in v3:
time: 117 us
  Pallas kernels  113 us (97%)
  local copies, waits for them, and re-layouts  3.7 us (3%)
    pallas_call x1, Pallas kernels, local(): pl.pallas_call(functools.partial(fused_body, n, fronts, cap, B), out_shap...  113 us
    unnamed x2, local copies, waits for them, and re-layouts  3.7 us

profile of v3, /device:TPU:1, one launch (start us, length us, event | category | flops | bytes accessed | tf_op | source)
XLA Modules:
  0.0 116.5 jit_solution(3666220201156367589)
XLA Ops:
  0.0 1.4 %copy.6.d_ref = s32[128,1]{1,0:T(8,128)} copy(s32[128,1]{0,1:T(1,128)} %param.6) | data formatting | bytes 1024 | tf_op args[1]
  1.4 112.8 %merge.1 = f32[256,1024]{1,0:T(8,128)} custom-call(f32[128,1024]{1,0:T(8,128)} %x_ref.1, s32[128,1]{1,0:T(8,128)} %copy.6.d_ref, f32[2,128,512]{2,1,0:T(8,128)} %ch_ref.1, s32[2,512]{1,0:T(2,128)} %cc_ref.1, f32[1,1024]{1,0:T(1,128)} %w_ref.1), custom_call_target="tpu_custom_call" | custom-call | tf_op jit(solution)/shard_map/merge/pallas_call | solution.py:326
  114.2 2.3 %copy.8 = f32[1,256,1024]{2,1,0:T(8,128)} copy(f32[1,256,1024]{2,1,0:T(8,128)} %bitcast.1) | data formatting | bytes 2097152
